TPU v7x, 32 devices: a whole 2x2x4 slice. The times are simulated.
32 devices in a mesh: tok: 16 (over z, y, core), cand: 2 (over x).
Axes of the slice: x: 2, y: 2, z: 4, core: 2. Of those that a mesh axis runs over, the one named last changes fastest.
Arguments:
- dec_hidden: bfloat16 [2, 16, 32, 2048], P(None, 'cand'), may hold values from -6 to 6
- enc_keys: bfloat16 [2, 2048, 2048], P(None, 'tok'), may hold values from -250 to 250
- enc_values: bfloat16 [2, 2048, 2048], P(None, 'tok'), may hold values from -72 to 72
- enc_lengths: int32 [2], replicated, may hold values from 512 to 2048, as said below
- cand_counts: int32 [2], replicated, may hold values from 4 to 16, as said below
- gold_ids: int32 [2, 16, 32], P(None, 'cand'), may hold values from 0 to 32127
- gain_cross: float32 [2048], replicated, may hold values from 0.25 to 1.75
- w_query: bfloat16 [2048, 2048], P('cand', 'tok'), may hold values from -0.125 to 0.125
- w_out: bfloat16 [2048, 2048], P('tok', 'cand'), may hold values from -0.125 to 0.125
- gain_ffn: float32 [2048], replicated, may hold values from 0.25 to 1.75
- w_in_gate: bfloat16 [2048, 5120], P('cand', 'tok'), may hold values from -0.125 to 0.125
- w_in_up: bfloat16 [2048, 5120], P('cand', 'tok'), may hold values from -0.125 to 0.125
- w_ffn_out: bfloat16 [5120, 2048], P('tok', 'cand'), may hold values from -0.25 to 0.25
- gain_final: float32 [2048], replicated, may hold values from 0.25 to 1.75
- w_vocab: bfloat16 [2048, 32128], P('cand', 'tok'), may hold values from -20 to 20
Outputs:
- cand_scores: float32 [2, 16], P(None, 'cand')
- best_score: float32 [2], replicated
Inputs may be any that keep to these rules, and one draw needn't show every extreme that they name: `enc_lengths`: some query has all 2048 encoder tokens live. `cand_counts`: some query has all 16 candidates live.
All inputs are finite; a program needn't handle non-finite values.
Results may differ from a plain program's by a relative error of at most 0.0014.
The roundings to bfloat16 on the way count: a program that leaves them out, or rounds other values in their place, can miss the bound.
Values may be sent and summed in bfloat16 or wider, within the bound.
A program may use at most 64 MiB of HBM per device.

v0:
```python
import functools

import jax
import jax.numpy as jnp
from jax import lax
from jax.experimental import pallas as pl
from jax.experimental.pallas import tpu as pltpu
from jax.sharding import PartitionSpec as P


HEAD_DIM = 64
MESH = pl.DeviceIdType.MESH

norm_eps = 0.25
BF = jnp.bfloat16
F32 = jnp.float32


def root_norm(values, gain):
    squares = jnp.mean(values * values, axis=-1, keepdims=True)
    return values * lax.rsqrt(squares + norm_eps) * gain


def dot32(left_side, piece):
    return jnp.dot(left_side, piece, preferred_element_type=F32)


def mix_kernel(n, pieces, sub, *refs):
    part = refs[:pieces]
    resid, gain = refs[pieces : pieces + 2]
    after, every = refs[pieces + 2 : pieces + 4]
    (
        send_c, recv_c, send_y, recv_y, send_z, recv_z,
        cs, cr, ys, yr, zs, zr, gzs, gzr, gys, gyr, gcs, gcr,
    ) = refs[pieces + 4 :]
    outer = n // 4
    width = send_c.shape[-1]
    chunks = pieces * sub
    me = lax.axis_index("tok")
    a, y, c = me // 4, (me // 2) % 2, me % 2
    core_peer = a * 4 + y * 2 + (1 - c)
    mid_peer = a * 4 + (1 - y) * 2 + c

    def outer_peer(k):
        return ((a + k) % outer) * 4 + y * 2 + c

    barrier = pltpu.get_barrier_semaphore()
    peers = [core_peer, mid_peer] + [outer_peer(k) for k in range(1, outer)]
    for peer in peers:
        pl.semaphore_signal(barrier, inc=1, device_id={"tok": peer}, device_id_type=MESH)

    def remote(src, dst, s, r, peer):
        return pltpu.make_async_remote_copy(
            src_ref=src, dst_ref=dst, send_sem=s, recv_sem=r,
            device_id={"tok": peer}, device_id_type=MESH,
        )

    def piece_of(ch):
        at = (ch % sub) * width
        return part[ch // sub], slice(at, at + width)

    copies = []
    for ch in range(chunks):
        ref, cols = piece_of(ch)
        for i in range(outer):
            for m in range(2):
                send_c[ch, i * 2 + m] = ref[i * 4 + m * 2 + (1 - c), :, cols].astype(BF)
        if ch == 0:
            pl.semaphore_wait(barrier, len(peers))
        cp = remote(send_c.at[ch], recv_c.at[ch], cs.at[ch], cr.at[ch], core_peer)
        cp.start()
        copies.append(cp)
    core_copies = list(copies)
    mid_copies = []
    for ch in range(chunks):
        ref, cols = piece_of(ch)
        core_copies[ch].wait_recv()
        for i in range(outer):
            other = 1 - y
            send_y[ch, i] = (
                ref[i * 4 + other * 2 + c, :, cols] + recv_c[ch, i * 2 + other].astype(F32)
            ).astype(BF)
        cp = remote(send_y.at[ch], recv_y.at[ch], ys.at[ch], yr.at[ch], mid_peer)
        cp.start()
        copies.append(cp)
        mid_copies.append(cp)

    def joined(ch, i):
        ref, cols = piece_of(ch)
        return (
            ref[i * 4 + y * 2 + c, :, cols]
            + recv_c[ch, i * 2 + y].astype(F32)
            + recv_y[ch, i].astype(F32)
        )

    outer_copies = []
    for ch in range(chunks):
        mid_copies[ch].wait_recv()
        row = []
        for k in range(1, outer):
            to = (a + k) % outer
            send_z[ch, k - 1] = joined(ch, to).astype(BF)
            cp = remote(
                send_z.at[ch, k - 1], recv_z.at[ch, k - 1],
                zs.at[ch, k - 1], zr.at[ch, k - 1], outer_peer(k),
            )
            cp.start()
            copies.append(cp)
            row.append(cp)
        outer_copies.append(row)
    for ch in range(chunks):
        total = joined(ch, a)
        for k in range(1, outer):
            outer_copies[ch][k - 1].wait_recv()
            total = total + recv_z[ch, k - 1].astype(F32)
        cols = slice(ch * width, (ch + 1) * width)
        after[:, cols] = resid[:, cols] + total
    values = after[...]
    every[me] = root_norm(values, gain[...]).astype(BF)

    gz, gy, gc = [], [], []
    for k in range(1, outer):
        cp = remote(every.at[me], every.at[me], gzs.at[k - 1], gzr.at[k - 1], outer_peer(k))
        cp.start()
        gz.append(cp)

    def block(k, m, e):
        return ((a + outer - k) % outer) * 4 + m * 2 + e

    def to_mid(k):
        b = block(k, y, c)
        cp = remote(every.at[b], every.at[b], gys.at[k], gyr.at[k], mid_peer)
        cp.start()
        gy.append(cp)

    def to_core(k, m, slot):
        b = block(k, m, c)
        cp = remote(every.at[b], every.at[b], gcs.at[slot], gcr.at[slot], core_peer)
        cp.start()
        gc.append(cp)

    to_mid(0)
    to_core(0, y, 0)
    for k in range(1, outer):
        gz[k - 1].wait_recv()
        to_mid(k)
        to_core(k, y, 2 * k)
    for k in range(outer):
        gy[k].wait_recv()
        to_core(k, 1 - y, 2 * k + 1)
    for cp in gc:
        cp.wait_recv()
    for cp in copies + gz + gy + gc:
        cp.wait_send()


def mix(parts, resid, gain, n, ident):
    pieces = len(parts)
    share, width = resid.shape
    sub = max(1, 4 // pieces)
    cw = width // pieces // sub
    chunks = pieces * sub
    outer = n // 4
    vm = pl.BlockSpec(memory_space=pltpu.VMEM)
    dma = pltpu.SemaphoreType.DMA
    parts = [p.reshape(n, share, width // pieces) for p in parts]
    return pl.pallas_call(
        functools.partial(mix_kernel, n, pieces, sub),
        out_shape=(
            jax.ShapeDtypeStruct((share, width), F32),
            jax.ShapeDtypeStruct((n, share, width), BF),
        ),
        in_specs=[vm] * (pieces + 2),
        out_specs=(vm, vm),
        scratch_shapes=[
            pltpu.VMEM((chunks, outer * 2, share, cw), BF),
            pltpu.VMEM((chunks, outer * 2, share, cw), BF),
            pltpu.VMEM((chunks, outer, share, cw), BF),
            pltpu.VMEM((chunks, outer, share, cw), BF),
            pltpu.VMEM((chunks, outer - 1, share, cw), BF),
            pltpu.VMEM((chunks, outer - 1, share, cw), BF),
            dma((chunks,)), dma((chunks,)), dma((chunks,)), dma((chunks,)),
            dma((chunks, outer - 1)), dma((chunks, outer - 1)),
            dma((outer - 1,)), dma((outer - 1,)),
            dma((outer,)), dma((outer,)), dma((2 * outer,)), dma((2 * outer,)),
        ],
        compiler_params=pltpu.CompilerParams(
            collective_id=ident, has_side_effects=True, vmem_limit_bytes=32 << 20
        ),
        cost_estimate=pl.CostEstimate(
            flops=10**7, bytes_accessed=100 * 10**6, transcendentals=0
        ),
    )(*parts, resid, gain.reshape(1, width))


def stats_kernel(n, mine, out, ss, rs):
    me = lax.axis_index("tok")
    barrier = pltpu.get_barrier_semaphore()
    for k in range(1, n):
        pl.semaphore_signal(
            barrier, inc=1, device_id={"tok": (me + k) % n}, device_id_type=MESH
        )
    out[me] = mine[...]
    pl.semaphore_wait(barrier, n - 1)
    copies = []
    for k in range(1, n):
        cp = pltpu.make_async_remote_copy(
            src_ref=mine, dst_ref=out.at[me], send_sem=ss.at[k - 1], recv_sem=rs.at[k - 1],
            device_id={"tok": (me + k) % n}, device_id_type=MESH,
        )
        cp.start()
        copies.append(cp)
    for cp in copies:
        cp.wait_recv()
    for cp in copies:
        cp.wait_send()


def gather_stats(mine, n):
    vm = pl.BlockSpec(memory_space=pltpu.VMEM)
    return pl.pallas_call(
        functools.partial(stats_kernel, n),
        out_shape=jax.ShapeDtypeStruct((n,) + mine.shape, F32),
        in_specs=[vm],
        out_specs=vm,
        scratch_shapes=[pltpu.SemaphoreType.DMA((n - 1,)), pltpu.SemaphoreType.DMA((n - 1,))],
        compiler_params=pltpu.CompilerParams(collective_id=3, has_side_effects=True),
        cost_estimate=pl.CostEstimate(flops=1000, bytes_accessed=10**7, transcendentals=0),
        name="stats",
    )(mine)


VOCAB_CHUNKS = 4


def body(
    dec_hidden,
    enc_keys,
    enc_values,
    enc_lengths,
    cand_counts,
    gold_ids,
    gain_cross,
    w_query,
    w_out,
    gain_ffn,
    w_in_gate,
    w_in_up,
    w_ffn_out,
    gain_final,
    w_vocab,
):
    query_count, cand_dev, length_tok, model_width = dec_hidden.shape
    src_dev = enc_keys.shape[1]
    n = lax.axis_size("tok")
    nc = lax.axis_size("cand")
    tok_index = lax.axis_index("tok")
    j = lax.axis_index("cand")
    rows = query_count * cand_dev * length_tok
    per_query = cand_dev * length_tok
    share = rows // n
    head_cols = w_query.shape[1]
    heads_dev = head_cols // HEAD_DIM
    kc = model_width // nc

    def shifted(value, p):
        return lax.ppermute(value, "cand", [((i + p) % nc, i) for i in range(nc)])

    def ring(w):
        return [w] + [shifted(w, p) for p in range(1, nc)]

    def rotate(value, axis):
        size = value.shape[axis] // nc
        return jnp.concatenate(
            [
                lax.dynamic_slice_in_dim(value, ((j + p) % nc) * size, size, axis)
                for p in range(nc)
            ],
            axis,
        )

    vocab_cols = w_vocab.shape[1]
    step = -(-vocab_cols // VOCAB_CHUNKS // 8) * 8
    edges = [min(i * step, vocab_cols) for i in range(VOCAB_CHUNKS + 1)]
    wq, wo = ring(w_query), ring(w_out)
    wg, wu, wd = ring(w_in_gate), ring(w_in_up), ring(w_ffn_out)
    wv = [ring(w_vocab[:, lo:hi]) for lo, hi in zip(edges, edges[1:])]

    split = nc if heads_dev % nc == 0 else 1
    hc = head_cols // split
    hpd = hc // HEAD_DIM

    def pick(value):
        v = value.reshape(query_count, src_dev, n, split, hc)
        at = j if split > 1 else 0
        return lax.dynamic_index_in_dim(v, at, 3, keepdims=False)

    kv = jnp.concatenate([pick(enc_keys), pick(enc_values)], -1).transpose(2, 0, 1, 3)
    kv = lax.all_to_all(kv, "tok", split_axis=0, concat_axis=0, tiled=True)
    kv = kv.transpose(1, 0, 2, 3).reshape(query_count, n * src_dev, 2 * hc)
    keys = kv[..., :hc].reshape(query_count, -1, hpd, HEAD_DIM)
    values = kv[..., hc:].reshape(query_count, -1, hpd, HEAD_DIM)

    x_rot = rotate(dec_hidden.reshape(rows, model_width), 1)
    gain_cross, gain_ffn, gain_final = (
        rotate(g, 0) for g in (gain_cross, gain_ffn, gain_final)
    )
    normed = root_norm(x_rot.astype(F32), gain_cross).astype(BF)

    def deep(left_side, shards):
        total = dot32(left_side[:, :kc], shards[0])
        for p in range(1, nc):
            total = total + dot32(left_side[:, p * kc : (p + 1) * kc], shards[p])
        return total

    query_local = deep(normed, wq).astype(BF)
    if split > 1:
        groups = []
        for p in range(nc):
            cols = lax.dynamic_slice_in_dim(query_local, ((j + nc - p) % nc) * hc, hc, 1)
            groups.append(cols if p == 0 else shifted(cols, p))
        query = jnp.stack(groups)
    else:
        query = query_local[None]
    ng = query.shape[0]
    query = query.reshape(ng, query_count, per_query, hpd, HEAD_DIM)
    query = query.transpose(1, 0, 2, 3, 4).reshape(query_count, ng * per_query, hpd, HEAD_DIM)

    live = (lax.iota(jnp.int32, n * src_dev)[None, :] < enc_lengths[:, None])[:, None, None, :]
    scores = jnp.einsum("brhd,bshd->bhrs", query, keys, preferred_element_type=F32)
    scores = jnp.where(live, scores, -1e30)
    row_max = jnp.max(scores, axis=-1, keepdims=True)
    weights = jnp.where(live, jnp.exp(scores - row_max), 0.0)
    denominator = jnp.sum(weights, axis=-1)
    mixed = jnp.einsum(
        "bhrs,bshd->brhd", weights.astype(BF), values, preferred_element_type=F32
    )
    attended = (mixed / denominator.transpose(0, 2, 1)[..., None]).astype(BF)
    attended = attended.reshape(query_count, ng, per_query, hc).transpose(1, 0, 2, 3)
    attended = attended.reshape(ng, rows, hc)
    if split > 1:
        heads = [attended[0]] + [
            lax.ppermute(attended[p], "cand", [(i, (i + p) % nc) for i in range(nc)])
            for p in range(1, nc)
        ]
        attended = jnp.concatenate(
            [lax.select_n((j + nc - b) % nc, *heads) if nc > 2 else jnp.where(j == b, heads[0], heads[1]) for b in range(nc)],
            axis=1,
        )
    else:
        attended = attended[0]

    resid = lax.dynamic_slice_in_dim(x_rot, tok_index * share, share, 0).astype(F32)
    after_cross, ffn_every = mix([dot32(attended, w) for w in wo], resid, gain_ffn, n, 1)
    ffn_every = ffn_every.reshape(rows, model_width)
    gate_part = deep(ffn_every, wg)
    up_part = deep(ffn_every, wu)
    hidden = (jax.nn.gelu(gate_part, approximate=True) * up_part).astype(BF)
    _, final_every = mix([dot32(hidden, w) for w in wd], after_cross, gain_final, n, 2)
    final_every = final_every.reshape(rows, model_width)

    gold_here = gold_ids.reshape(rows) - tok_index * vocab_cols
    maxima, sums, golds = [], [], []
    for lo, hi, shards in zip(edges, edges[1:], wv):
        logits = deep(final_every, shards)
        matches = lo + lax.iota(jnp.int32, hi - lo)[None, :] == gold_here[:, None]
        golds.append(jnp.sum(jnp.where(matches, logits, 0.0), axis=1))
        maxima.append(jnp.max(logits, axis=1))
        sums.append(jnp.sum(jnp.exp(logits - maxima[-1][:, None]), axis=1))
    local_max = functools.reduce(jnp.maximum, maxima)
    local_sum = sum(t * jnp.exp(m - local_max) for t, m in zip(sums, maxima))
    gold_local = sum(golds)
    stats = gather_stats(jnp.stack([local_max, local_sum, gold_local]).reshape(-1, 128), n)
    stats = stats.reshape(n, 3, rows)
    global_max = jnp.max(stats[:, 0], axis=0)
    sum_exp = jnp.sum(stats[:, 1] * jnp.exp(stats[:, 0] - global_max), axis=0)
    gold_logit = jnp.sum(stats[:, 2], axis=0)
    logprob = gold_logit - global_max - jnp.log(sum_exp)
    per_cand = jnp.mean(logprob.reshape(query_count, cand_dev, length_tok), axis=2)
    cand_index = j * cand_dev + lax.iota(jnp.int32, cand_dev)
    valid_cand = cand_index[None, :] < cand_counts[:, None]
    cand_scores = jnp.where(valid_cand, per_cand, 0.0)
    best_local = jnp.max(jnp.where(valid_cand, per_cand, -1e30), axis=1)
    best_score = lax.pmax(best_local, "cand")
    return (cand_scores, best_score)


def solution(mesh):
    in_specs = (
        P(None, "cand", None, None),
        P(None, "tok", None),
        P(None, "tok", None),
        P(),
        P(),
        P(None, "cand", None),
        P(),
        P("cand", "tok"),
        P("tok", "cand"),
        P(),
        P("cand", "tok"),
        P("cand", "tok"),
        P("tok", "cand"),
        P(),
        P("cand", "tok"),
    )
    out_specs = (P(None, "cand"), P())

    return jax.shard_map(body, mesh=mesh, in_specs=in_specs, out_specs=out_specs, check_vma=False)
```

profile of v0, /device:TPU:0, one launch (start us, length us, event | category | flops | bytes accessed | tf_op | source)
XLA Modules:
  0.0 206.6 jit_solution(6727861525215170206)
XLA Ops:
  0.6 3.0 %collective-permute-start = (bf16[1024,128]{1,0:T(8,128)(2,1)}, bf16[1024,128]{1,0:T(8,128)(2,1)}, u32[]{:S(2)}, u32[]{:S(2)}) collective-permute-start(bf16[1024,128]{1,0:T(8,128)(2,1)} %param.22), channel_id=1, source_target_pairs={{1,0},{0,1},{3,2},{2,3},{5,4},{4,5},{7,6},{6,7},{9,8},{8,9},{11,10... | collective-permute-start | bytes 786440 | tf_op jit(solution)/shard_map/ppermute | solution.py:267
  3.7 1.6 copy.39
  7.3 5.9 %all-to-all-start = ((bf16[16,2,128,128]{2,3,1,0:T(8,128)(2,1)}), bf16[16,2,128,128]{2,3,1,0:T(8,128)(2,1)S(1)}, u32[]{:S(2)}, u32[]{:S(2)}) async-start(bf16[16,2,128,128]{2,3,1,0:T(8,128)(2,1)} %copy.41), calls=%async_computation | async-start | bytes 2097152 | tf_op jit(solution)/shard_map/all_to_all | solution.py:299
  13.8 1.5 collective-permute-start.4
  15.8 1.5 collective-permute-start.6
  17.3 1.7 constant_dynamic-slice_fusion.3
  19.8 3.6 %fusion.82 = (bf16[1024,504]{0,1:T(8,128)(2,1)}, bf16[1024,504]{0,1:T(8,128)(2,1)}, bf16[1024,504]{0,1:T(8,128)(2,1)}) fusion(bf16[1024,2008]{0,1:T(8,128)(2,1)} %param.29), kind=kLoop, calls=%fused_computation.122 | loop fusion | bytes 6193152 | tf_op jit(solution)/shard_map/slice | solution.py:287
  23.5 2.2 %slice.75 = bf16[1024,496]{0,1:T(8,128)(2,1)} slice(bf16[1024,2008]{0,1:T(8,128)(2,1)} %param.29), slice={[0:1024], [1512:2008]} | slice | bytes 2031616 | tf_op jit(solution)/shard_map/slice | solution.py:287
  29.5 36.1 %collective-permute-done.1 = bf16[512,64]{0,1:T(8,128)(2,1)S(1)} collective-permute-done((bf16[512,64]{0,1:T(8,128)(2,1)S(1)}, bf16[512,64]{0,1:T(8,128)(2,1)S(1)}, u32[]{:S(2)}, u32[]{:S(2)}) %collective-permute-start.1) | collective-permute-done | bytes 65568 | tf_op jit(solution)/shard_map/ppermute | solution.py:267
  66.2 4.7 %fusion.87 = (f32[2,512]{1,0:T(2,128)S(1)}, bf16[2,512,2048]{2,1,0:T(8,128)(2,1)}) fusion(pred[2,2048]{1,0:T(4,128)(4,1)S(1)} %iota_compare_fusion.1, bf16[2,512,64]{1,2,0:T(8,128)(2,1)S(1)} %reshape.291, bf16[2,2048,128]{1,2,0:T(8,128)(2,1)S(1)} %copy_bitcast_fusion), kind=kOutput, calls=%fused_computation.127 | convolution fusion | flops 278923264 | bytes 4870144 | tf_op jit(solution)/shard_map/sub | solution.py:333
  70.9 3.7 %fusion.23 = bf16[2,512,1,64]{1,3,0,2:T(8,128)(2,1)S(1)} fusion(bf16[2,512,2048]{2,1,0:T(8,128)(2,1)} %get-tuple-element.46, bf16[2,2048,128]{1,2,0:T(8,128)(2,1)S(1)} %copy_bitcast_fusion, f32[2,512]{1,0:T(2,128)S(1)} %get-tuple-element.45), kind=kOutput, calls=%fused_computation.29 | convolution fusion | flops 268566528 | bytes 4853760 | tf_op jit(solution)/shard_map/bhrs,bshd->brhd/dot_general | solution.py:335
  75.5 3.7 %collective-permute-done.2 = bf16[512,64]{0,1:T(8,128)(2,1)S(1)} collective-permute-done((bf16[512,64]{0,1:T(8,128)(2,1)S(1)}, bf16[512,64]{0,1:T(8,128)(2,1)S(1)}, u32[]{:S(2)}, u32[]{:S(2)}) %collective-permute-start.2) | collective-permute-done | bytes 65568 | tf_op jit(solution)/shard_map/ppermute | solution.py:343
  81.2 1.5 collective-permute-start.9
  84.2 40.8 %shard_map.158 = (f32[32,2048]{1,0:T(8,128)S(1)}, bf16[16,32,2048]{2,1,0:T(8,128)(2,1)S(1)}) custom-call(f32[16,32,1024]{2,1,0:T(8,128)S(1)} %bitcast.106, f32[16,32,1024]{2,1,0:T(8,128)S(1)} %bitcast.108, f32[32,2048]{1,0:T(8,128)S(1)} %fusion.67.refs_2_, f32[1,2048]{1,0:T(1,128)S(1)} %bitcast.114), custom_call_target="tpu_custom_call" | custom-call | flops 10000000 | bytes 100000000 | tf_op jit(solution)/shard_map/pallas_call | solution.py:167
  125.0 1.7 fusion.35
  127.3 1.8 fusion.55
  129.1 1.7 fusion.33
  130.8 1.6 collective-permute-start.10
  132.4 1.6 fusion.12
  134.0 1.8 fusion.96
  135.8 1.8 fusion.97
  137.7 43.0 %shard_map.159 = (f32[32,2048]{1,0:T(8,128)}, bf16[16,32,2048]{2,1,0:T(8,128)(2,1)S(1)}) custom-call(f32[16,32,1024]{2,1,0:T(8,128)S(1)} %bitcast.107, f32[16,32,1024]{2,1,0:T(8,128)S(1)} %bitcast.109, f32[32,2048]{1,0:T(8,128)S(1)} %get-tuple-element.6.refs_2_, f32[1,2048]{1,0:T(1,128)S(1)} %bitcast.115), custom_call_target="tpu_custom_call" | custom-call | flops 10000000 | bytes 100000000 | tf_op jit(solution)/shard_map/pallas_call | solution.py:167
  188.5 10.7 %stats.1 = f32[16,12,128]{2,1,0:T(8,128)} custom-call(f32[12,128]{1,0:T(8,128)} %reshape.301.mine), custom_call_target="tpu_custom_call" | custom-call | flops 1000 | bytes 10000000 | tf_op jit(solution)/shard_map/stats/pallas_call | solution.py:221
  201.2 5.4 %pmax.7 = f32[2]{0:T(128)} all-reduce(f32[2]{0:T(128)S(1)} %get-tuple-element.39), channel_id=1, replica_groups=mesh['tok'=16,'cand'=2] {'cand'}, use_global_device_ids=true, to_apply=%region_20.21 | all-reduce | flops 2 | bytes 16 | tf_op jit(solution)/shard_map/pmax | solution.py:384
  (99 shorter events, 22.6 us)
Async XLA Ops:
  0.6 4.7 %copy-start.1 = (bf16[2,128,2048]{2,1,0:T(8,128)(2,1)S(1)}, bf16[2,128,2048]{2,1,0:T(8,128)(2,1)}, u32[]{:S(2)}) copy-start(bf16[2,128,2048]{2,1,0:T(8,128)(2,1)} %param.17) | copy-start | bytes 3145732
  0.6 26.7 %collective-permute-start = (bf16[1024,128]{1,0:T(8,128)(2,1)}, bf16[1024,128]{1,0:T(8,128)(2,1)}, u32[]{:S(2)}, u32[]{:S(2)}) collective-permute-start(bf16[1024,128]{1,0:T(8,128)(2,1)} %param.22), channel_id=1, source_target_pairs={{1,0},{0,1},{3,2},{2,3},{5,4},{4,5},{7,6},{6,7},{9,8},{8,9},{11,10... | collective-permute-start | bytes 786440 | tf_op jit(solution)/shard_map/ppermute | solution.py:267
  7.3 58.8 %all-to-all-start = ((bf16[16,2,128,128]{2,3,1,0:T(8,128)(2,1)}), bf16[16,2,128,128]{2,3,1,0:T(8,128)(2,1)S(1)}, u32[]{:S(2)}, u32[]{:S(2)}) async-start(bf16[16,2,128,128]{2,3,1,0:T(8,128)(2,1)} %copy.41), calls=%async_computation | async-start | bytes 2097152 | tf_op jit(solution)/shard_map/all_to_all | solution.py:299
  13.2 68.0 %collective-permute-start.3 = (bf16[128,1024]{1,0:T(8,128)(2,1)}, bf16[128,1024]{1,0:T(8,128)(2,1)}, u32[]{:S(2)}, u32[]{:S(2)}) collective-permute-start(bf16[128,1024]{1,0:T(8,128)(2,1)} %param.23), channel_id=1, source_target_pairs={{1,0},{0,1},{3,2},{2,3},{5,4},{4,5},{7,6},{6,7},{9,8},{8,9},{11,10... | collective-permute-start | bytes 786440 | tf_op jit(solution)/shard_map/ppermute | solution.py:267
  13.8 112.9 %collective-permute-start.4 = (bf16[1024,320]{0,1:T(8,128)(2,1)}, bf16[1024,320]{0,1:T(8,128)(2,1)}, u32[]{:S(2)}, u32[]{:S(2)}) collective-permute-start(bf16[1024,320]{0,1:T(8,128)(2,1)} %param.25), channel_id=1, source_target_pairs={{1,0},{0,1},{3,2},{2,3},{5,4},{4,5},{7,6},{6,7},{9,8},{8,9},{11,10... | collective-permute-start | bytes 1966088 | tf_op jit(solution)/shard_map/ppermute | solution.py:267
  15.3 115.5 %collective-permute-start.5 = (bf16[1024,320]{0,1:T(8,128)(2,1)}, bf16[1024,320]{0,1:T(8,128)(2,1)}, u32[]{:S(2)}, u32[]{:S(2)}) collective-permute-start(bf16[1024,320]{0,1:T(8,128)(2,1)} %param.26), channel_id=1, source_target_pairs={{1,0},{0,1},{3,2},{2,3},{5,4},{4,5},{7,6},{6,7},{9,8},{8,9},{11,10... | collective-permute-start | bytes 1966088 | tf_op jit(solution)/shard_map/ppermute | solution.py:267
  15.8 120.0 %collective-permute-start.6 = (bf16[320,1024]{1,0:T(8,128)(2,1)}, bf16[320,1024]{1,0:T(8,128)(2,1)}, u32[]{:S(2)}, u32[]{:S(2)}) collective-permute-start(bf16[320,1024]{1,0:T(8,128)(2,1)} %param.27), channel_id=1, source_target_pairs={{1,0},{0,1},{3,2},{2,3},{5,4},{4,5},{7,6},{6,7},{9,8},{8,9},{11,10... | collective-permute-start | bytes 1966088 | tf_op jit(solution)/shard_map/ppermute | solution.py:267
  19.8 3.6 %copy-start.9 = (f32[2048]{0:T(1024)S(1)}, f32[2048]{0:T(1024)}, u32[]{:S(2)}) copy-start(f32[2048]{0:T(1024)} %param.28) | copy-start | bytes 24580
  19.8 3.6 %copy-start.10 = (f32[2048]{0:T(1024)S(1)}, f32[2048]{0:T(1024)}, u32[]{:S(2)}) copy-start(f32[2048]{0:T(1024)} %param.24) | copy-start | bytes 24580
  19.8 3.6 %copy-start.8 = (s32[2,8,32]{2,1,0:T(8,128)S(1)}, s32[2,8,32]{2,1,0:T(8,128)}, u32[]{:S(2)}) copy-start(s32[2,8,32]{2,1,0:T(8,128)} %param.20) | copy-start | bytes 6148
  23.4 2.4 %copy-start.11 = (s32[2]{0:T(128)S(1)}, s32[2]{0:T(128)}, u32[]{:S(2)}) copy-start(s32[2]{0:T(128)} %param.18) | copy-start | bytes 28
  25.9 1.0 copy-start.6
  28.8 36.8 %collective-permute-start.1 = (bf16[512,64]{0,1:T(8,128)(2,1)S(1)}, bf16[512,64]{0,1:T(8,128)(2,1)S(1)}, u32[]{:S(2)}, u32[]{:S(2)}) collective-permute-start(bf16[512,64]{0,1:T(8,128)(2,1)S(1)} %get-tuple-element.30), channel_id=1, source_target_pairs={{1,0},{0,1},{3,2},{2,3},{5,4},{4,5},{7,6},{6,7},{9,8},{8,9},{11,10... | collective-permute-start | bytes 196616 | tf_op jit(solution)/shard_map/ppermute | solution.py:267
  70.9 8.3 %copy-start.4 = (bf16[1024,504]{0,1:T(8,128)(2,1)S(1)}, bf16[1024,504]{0,1:T(8,128)(2,1)}, u32[]{:S(2)}) copy-start(bf16[1024,504]{0,1:T(8,128)(2,1)} %get-tuple-element.19) | copy-start | bytes 3096580
  74.6 6.6 %copy-start.3 = (bf16[1024,504]{0,1:T(8,128)(2,1)S(1)}, bf16[1024,504]{0,1:T(8,128)(2,1)}, u32[]{:S(2)}) copy-start(bf16[1024,504]{0,1:T(8,128)(2,1)} %get-tuple-element.20) | copy-start | bytes 3096580
  74.9 4.3 %collective-permute-start.2 = (bf16[512,64]{0,1:T(8,128)(2,1)S(1)}, bf16[512,64]{0,1:T(8,128)(2,1)S(1)}, u32[]{:S(2)}, u32[]{:S(2)}) collective-permute-start(bf16[512,64]{0,1:T(8,128)(2,1)S(1)} %bitcast.123), channel_id=1, source_target_pairs={{0,1},{1,0},{2,3},{3,2},{4,5},{5,4},{6,7},{7,6},{8,9},{9,8},{10,11... | collective-permute-start | bytes 196616 | tf_op jit(solution)/shard_map/ppermute | solution.py:343
  79.3 105.4 %collective-permute-start.7 = (bf16[1024,504]{0,1:T(8,128)(2,1)S(1)}, bf16[1024,504]{0,1:T(8,128)(2,1)S(1)}, u32[]{:S(2)}, u32[]{:S(2)}) collective-permute-start(bf16[1024,504]{0,1:T(8,128)(2,1)S(1)} %copy-done.4), channel_id=1, source_target_pairs={{1,0},{0,1},{3,2},{2,3},{5,4},{4,5},{7,6},{6,7},{9,8},{8,9},{11,10... | collective-permute-start | bytes 3096584 | tf_op jit(solution)/shard_map/ppermute | solution.py:267
  81.2 104.2 %collective-permute-start.9 = (bf16[1024,504]{0,1:T(8,128)(2,1)S(1)}, bf16[1024,504]{0,1:T(8,128)(2,1)S(1)}, u32[]{:S(2)}, u32[]{:S(2)}) collective-permute-start(bf16[1024,504]{0,1:T(8,128)(2,1)S(1)} %copy-done.3), channel_id=1, source_target_pairs={{1,0},{0,1},{3,2},{2,3},{5,4},{4,5},{7,6},{6,7},{9,8},{8,9},{11,10... | collective-permute-start | bytes 3096584 | tf_op jit(solution)/shard_map/ppermute | solution.py:267
  125.0 1.7 copy-start.2
  126.7 59.5 %collective-permute-start.8 = (bf16[1024,504]{0,1:T(8,128)(2,1)S(1)}, bf16[1024,504]{0,1:T(8,128)(2,1)S(1)}, u32[]{:S(2)}, u32[]{:S(2)}) collective-permute-start(bf16[1024,504]{0,1:T(8,128)(2,1)S(1)} %copy-done.2), channel_id=1, source_target_pairs={{1,0},{0,1},{3,2},{2,3},{5,4},{4,5},{7,6},{6,7},{9,8},{8,9},{11,10... | collective-permute-start | bytes 3096584 | tf_op jit(solution)/shard_map/ppermute | solution.py:267
  129.1 1.7 copy-start.5
  130.8 50.6 %collective-permute-start.10 = (bf16[1024,496]{0,1:T(8,128)(2,1)S(1)}, bf16[1024,496]{0,1:T(8,128)(2,1)S(1)}, u32[]{:S(2)}, u32[]{:S(2)}) collective-permute-start(bf16[1024,496]{0,1:T(8,128)(2,1)S(1)} %copy-done.5), channel_id=1, source_target_pairs={{1,0},{0,1},{3,2},{2,3},{5,4},{4,5},{7,6},{6,7},{9,8},{8,9},{11,10... | collective-permute-start | bytes 3047432 | tf_op jit(solution)/shard_map/ppermute | solution.py:267
  137.7 43.0 %copy-start = (bf16[1024,2008]{0,1:T(8,128)(2,1)S(1)}, bf16[1024,2008]{0,1:T(8,128)(2,1)}, u32[]{:S(2)}) copy-start(bf16[1024,2008]{0,1:T(8,128)(2,1)} %param.29) | copy-start | bytes 12337156
  187.0 13.5 %copy-start.12 = (s32[2]{0:T(128)S(1)}, s32[2]{0:T(128)}, u32[]{:S(2)}) copy-start(s32[2]{0:T(128)} %param.19) | copy-start | bytes 28
  (1 other events, 0.7 us)
where the time goes:
time: 207 us
  Pallas kernels  94.5 us (46%)
  waiting for transfers between devices  39.9 us (19%)
  matrix products  29.5 us (14%)
  starting transfers between devices  18.5 us (9%)
  local copies, waits for them, and re-layouts  14.1 us (7%)
  blocking collectives  5.43 us (3%)
  other arithmetic  3.55 us (2%)
    pallas_call x2, Pallas kernels, mix(): pl.pallas_call(functools.partial(mix_kernel, n, pieces, sub), out_shape=(...  83.8 us
    ppermute x10, waiting for transfers between devices, shifted(): return lax.ppermute(value, 'cand', [((i + p) % nc, i) for i in range(nc)])  36.1 us
    dot_general x18, matrix products, dot32(): return jnp.dot(left_side, piece, preferred_element_type=F32)  21.1 us
    ppermute x10, starting transfers between devices, shifted(): return lax.ppermute(value, 'cand', [((i + p) % nc, i) for i in range(nc)])  12 us
    pallas_call x1, Pallas kernels, gather_stats(): pl.pallas_call(functools.partial(stats_kernel, n), out_shape=jax.ShapeDty...  10.7 us
    all_to_all x1, starting transfers between devices, body(): kv = lax.all_to_all(kv, 'tok', split_axis=0, concat_axis=0, tiled=True)  5.94 us
    slice x2, local copies, waits for them, and re-layouts, body(): wv = [ring(w_vocab[:, lo:hi]) for lo, hi in zip(edges, edges[1:])]  5.82 us
    pmax x1, blocking collectives, body(): best_score = lax.pmax(best_local, 'cand')  5.43 us
  transfers between devices with their start and end apart: 12, of which 2 were waited for; matrix products, arithmetic and copies ran while one was open for 20% of the time, Pallas kernels for 41%

commit v1 on v0

--- a/solution.py
+++ b/solution.py
@@ -193,41 +193,93 @@
     )(*parts, resid, gain.reshape(1, width))
 
 
-def stats_kernel(n, mine, out, ss, rs):
-    me = lax.axis_index("tok")
+def score_kernel(n, nc, per, length, counts, mine, out, best, got, best_got, ss, rs, bs, br):
+    me, j = lax.axis_index("tok"), lax.axis_index("cand")
     barrier = pltpu.get_barrier_semaphore()
     for k in range(1, n):
         pl.semaphore_signal(
             barrier, inc=1, device_id={"tok": (me + k) % n}, device_id_type=MESH
         )
-    out[me] = mine[...]
-    pl.semaphore_wait(barrier, n - 1)
+    for p in range(1, nc):
+        pl.semaphore_signal(
+            barrier, inc=1, device_id={"cand": (j + p) % nc}, device_id_type=MESH
+        )
+    got[me] = mine[...]
+    pl.semaphore_wait(barrier, n + nc - 2)
     copies = []
     for k in range(1, n):
         cp = pltpu.make_async_remote_copy(
-            src_ref=mine, dst_ref=out.at[me], send_sem=ss.at[k - 1], recv_sem=rs.at[k - 1],
+            src_ref=mine, dst_ref=got.at[me], send_sem=ss.at[k - 1], recv_sem=rs.at[k - 1],
             device_id={"tok": (me + k) % n}, device_id_type=MESH,
         )
         cp.start()
         copies.append(cp)
     for cp in copies:
         cp.wait_recv()
-    for cp in copies:
+    lines = mine.shape[0] // 2
+    every = got[...]
+    parts = every[:, :lines]
+    top = jnp.max(parts, axis=0)
+    total = top + jnp.log(jnp.sum(jnp.exp(parts - top), axis=0))
+    logprob = jnp.sum(every[:, lines:], axis=0) - total
+    per_line = 128 // length
+    group = lax.broadcasted_iota(jnp.int32, (lines, 128), 1) // length
+    line = lax.broadcasted_iota(jnp.int32, (lines, 128), 0)
+    mean = jnp.zeros((lines, 128), F32)
+    for g in range(per_line):
+        held = group == g
+        value = jnp.sum(jnp.where(held, logprob, 0.0), axis=1, keepdims=True) / length
+        mean = jnp.where(held, value, mean)
+    which = line * per_line + group
+    place = j * per + which % per
+    owner = which // per
+    queries = lines * per_line // per
+    row = lax.broadcasted_iota(jnp.int32, (8, 128), 0)
+    tops = jnp.full((8, 128), -1e30, F32)
+    scores = jnp.zeros((lines, 128), F32)
+    for b in range(queries):
+        valid = (owner == b) & (place < counts[b])
+        scores = jnp.where(valid, mean, scores)
+        high = jnp.max(jnp.where(valid, mean, -1e30), axis=(0, 1), keepdims=True)
+        tops = jnp.where(row == b, high, tops)
+    out[...] = scores
+    best_got[j] = tops
+    more = []
+    for p in range(1, nc):
+        cp = pltpu.make_async_remote_copy(
+            src_ref=best_got.at[j], dst_ref=best_got.at[j],
+            send_sem=bs.at[p - 1], recv_sem=br.at[p - 1],
+            device_id={"cand": (j + p) % nc}, device_id_type=MESH,
+        )
+        cp.start()
+        more.append(cp)
+    for cp in more:
+        cp.wait_recv()
+    best[...] = jnp.max(best_got[...], axis=0)
+    for cp in copies + more:
         cp.wait_send()
 
 
-def gather_stats(mine, n):
+def final_scores(mine, counts, n, nc, per, length):
     vm = pl.BlockSpec(memory_space=pltpu.VMEM)
+    dma = pltpu.SemaphoreType.DMA
     return pl.pallas_call(
-        functools.partial(stats_kernel, n),
-        out_shape=jax.ShapeDtypeStruct((n,) + mine.shape, F32),
-        in_specs=[vm],
-        out_specs=vm,
-        scratch_shapes=[pltpu.SemaphoreType.DMA((n - 1,)), pltpu.SemaphoreType.DMA((n - 1,))],
+        functools.partial(score_kernel, n, nc, per, length),
+        out_shape=(
+            jax.ShapeDtypeStruct((mine.shape[0] // 2, 128), F32),
+            jax.ShapeDtypeStruct((8, 128), F32),
+        ),
+        in_specs=[pl.BlockSpec(memory_space=pltpu.SMEM), vm],
+        out_specs=(vm, vm),
+        scratch_shapes=[
+            pltpu.VMEM((n,) + mine.shape, F32),
+            pltpu.VMEM((nc, 8, 128), F32),
+            dma((n - 1,)), dma((n - 1,)), dma((nc - 1,)), dma((nc - 1,)),
+        ],
         compiler_params=pltpu.CompilerParams(collective_id=3, has_side_effects=True),
         cost_estimate=pl.CostEstimate(flops=1000, bytes_accessed=10**7, transcendentals=0),
-        name="stats",
-    )(mine)
+        name="score",
+    )(counts, mine)
 
 
 VOCAB_CHUNKS = 4
@@ -370,18 +422,12 @@
     local_max = functools.reduce(jnp.maximum, maxima)
     local_sum = sum(t * jnp.exp(m - local_max) for t, m in zip(sums, maxima))
     gold_local = sum(golds)
-    stats = gather_stats(jnp.stack([local_max, local_sum, gold_local]).reshape(-1, 128), n)
-    stats = stats.reshape(n, 3, rows)
-    global_max = jnp.max(stats[:, 0], axis=0)
-    sum_exp = jnp.sum(stats[:, 1] * jnp.exp(stats[:, 0] - global_max), axis=0)
-    gold_logit = jnp.sum(stats[:, 2], axis=0)
-    logprob = gold_logit - global_max - jnp.log(sum_exp)
-    per_cand = jnp.mean(logprob.reshape(query_count, cand_dev, length_tok), axis=2)
-    cand_index = j * cand_dev + lax.iota(jnp.int32, cand_dev)
-    valid_cand = cand_index[None, :] < cand_counts[:, None]
-    cand_scores = jnp.where(valid_cand, per_cand, 0.0)
-    best_local = jnp.max(jnp.where(valid_cand, per_cand, -1e30), axis=1)
-    best_score = lax.pmax(best_local, "cand")
+    lse_local = local_max + jnp.log(local_sum)
+    scores_all, best_all = final_scores(
+        jnp.stack([lse_local, gold_local]).reshape(-1, 128), cand_counts, n, nc, cand_dev, length_tok
+    )
+    cand_scores = scores_all.reshape(query_count, cand_dev, length_tok)[:, :, 0]
+    best_score = best_all[:query_count, 0]
     return (cand_scores, best_score)
 
 

time: 207 us -> 205 us (level)
  blocking collectives: 5.43 us -> 0 us
  Pallas kernels: 94.5 us -> 97.4 us
    pmax x1 -> x0, blocking collectives: 5.43 us -> none  [body(): best_score = lax.pmax(best_local, 'cand')]
    pallas_call x1, Pallas kernels: 10.7 us -> 13.6 us  [final_scores(): pl.pallas_call(functools.partial(score_kernel, n, nc, per, length), out_s...]
  transfers between devices with their start and end apart: 12 -> 12, of which waited for: 2 -> 2; matrix products, arithmetic and copies ran while one was open for 20% -> 21% of each run, Pallas kernels for 41% -> 41%
where the time goes in v1:
time: 205 us
  Pallas kernels  97.4 us (48%)
  waiting for transfers between devices  39.9 us (19%)
  matrix products  29.4 us (14%)
  starting transfers between devices  18.5 us (9%)
  local copies, waits for them, and re-layouts  15.7 us (8%)
  other arithmetic  2.57 us (1%)
    pallas_call x2, Pallas kernels, mix(): pl.pallas_call(functools.partial(mix_kernel, n, pieces, sub), out_shape=(...  83.8 us
    ppermute x10, waiting for transfers between devices, shifted(): return lax.ppermute(value, 'cand', [((i + p) % nc, i) for i in range(nc)])  36.1 us
    dot_general x18, matrix products, dot32(): return jnp.dot(left_side, piece, preferred_element_type=F32)  21 us
    pallas_call x1, Pallas kernels, final_scores(): pl.pallas_call(functools.partial(score_kernel, n, nc, per, length), out_s...  13.6 us
    ppermute x10, starting transfers between devices, shifted(): return lax.ppermute(value, 'cand', [((i + p) % nc, i) for i in range(nc)])  12 us
    all_to_all x1, starting transfers between devices, body(): kv = lax.all_to_all(kv, 'tok', split_axis=0, concat_axis=0, tiled=True)  5.94 us
    slice x2, local copies, waits for them, and re-layouts, body(): wv = [ring(w_vocab[:, lo:hi]) for lo, hi in zip(edges, edges[1:])]  5.82 us
    sub x1, matrix products, body(): weights = jnp.where(live, jnp.exp(scores - row_max), 0.0)  4.73 us
  transfers between devices with their start and end apart: 12, of which 2 were waited for; matrix products, arithmetic and copies ran while one was open for 21% of the time, Pallas kernels for 41%

profile of v1, /device:TPU:0, one launch (start us, length us, event | category | flops | bytes accessed | tf_op | source)
XLA Modules:
  0.0 204.7 jit_solution(5978641365276276405)
XLA Ops:
  0.6 3.0 %collective-permute-start = (bf16[1024,128]{1,0:T(8,128)(2,1)}, bf16[1024,128]{1,0:T(8,128)(2,1)}, u32[]{:S(2)}, u32[]{:S(2)}) collective-permute-start(bf16[1024,128]{1,0:T(8,128)(2,1)} %param.22), channel_id=1, source_target_pairs={{1,0},{0,1},{3,2},{2,3},{5,4},{4,5},{7,6},{6,7},{9,8},{8,9},{11,10... | collective-permute-start | bytes 786440 | tf_op jit(solution)/shard_map/ppermute | solution.py:319
  3.7 1.6 copy.32
  7.3 5.9 %all-to-all-start = ((bf16[16,2,128,128]{2,3,1,0:T(8,128)(2,1)}), bf16[16,2,128,128]{2,3,1,0:T(8,128)(2,1)S(1)}, u32[]{:S(2)}, u32[]{:S(2)}) async-start(bf16[16,2,128,128]{2,3,1,0:T(8,128)(2,1)} %copy.34), calls=%async_computation | async-start | bytes 2097152 | tf_op jit(solution)/shard_map/all_to_all | solution.py:351
  13.8 1.5 collective-permute-start.4
  15.8 1.5 collective-permute-start.6
  17.3 1.7 constant_dynamic-slice_fusion.3
  19.8 3.6 %fusion.77 = (bf16[1024,504]{0,1:T(8,128)(2,1)}, bf16[1024,504]{0,1:T(8,128)(2,1)}, bf16[1024,504]{0,1:T(8,128)(2,1)}) fusion(bf16[1024,2008]{0,1:T(8,128)(2,1)} %param.29), kind=kLoop, calls=%fused_computation.110 | loop fusion | bytes 6193152 | tf_op jit(solution)/shard_map/slice | solution.py:339
  23.5 2.2 %slice.71 = bf16[1024,496]{0,1:T(8,128)(2,1)} slice(bf16[1024,2008]{0,1:T(8,128)(2,1)} %param.29), slice={[0:1024], [1512:2008]} | slice | bytes 2031616 | tf_op jit(solution)/shard_map/slice | solution.py:339
  27.4 1.4 fusion.22
  29.5 36.1 %collective-permute-done.1 = bf16[512,64]{0,1:T(8,128)(2,1)S(1)} collective-permute-done((bf16[512,64]{0,1:T(8,128)(2,1)S(1)}, bf16[512,64]{0,1:T(8,128)(2,1)S(1)}, u32[]{:S(2)}, u32[]{:S(2)}) %collective-permute-start.1) | collective-permute-done | bytes 65568 | tf_op jit(solution)/shard_map/ppermute | solution.py:319
  66.2 4.7 %fusion.82 = (f32[2,512]{1,0:T(2,128)S(1)}, bf16[2,512,2048]{2,1,0:T(8,128)(2,1)}) fusion(pred[2,2048]{1,0:T(4,128)(4,1)S(1)} %iota_compare_fusion.1, bf16[2,512,64]{1,2,0:T(8,128)(2,1)S(1)} %reshape.268, bf16[2,2048,128]{1,2,0:T(8,128)(2,1)S(1)} %copy_bitcast_fusion), kind=kOutput, calls=%fused_computation.115 | convolution fusion | flops 278923264 | bytes 4870144 | tf_op jit(solution)/shard_map/sub | solution.py:385
  70.9 3.7 %fusion.23 = bf16[2,512,1,64]{1,3,0,2:T(8,128)(2,1)S(1)} fusion(bf16[2,512,2048]{2,1,0:T(8,128)(2,1)} %get-tuple-element.42, bf16[2,2048,128]{1,2,0:T(8,128)(2,1)S(1)} %copy_bitcast_fusion, f32[2,512]{1,0:T(2,128)S(1)} %get-tuple-element.41), kind=kOutput, calls=%fused_computation.29 | convolution fusion | flops 268566528 | bytes 4853760 | tf_op jit(solution)/shard_map/bhrs,bshd->brhd/dot_general | solution.py:387
  75.5 3.7 %collective-permute-done.2 = bf16[512,64]{0,1:T(8,128)(2,1)S(1)} collective-permute-done((bf16[512,64]{0,1:T(8,128)(2,1)S(1)}, bf16[512,64]{0,1:T(8,128)(2,1)S(1)}, u32[]{:S(2)}, u32[]{:S(2)}) %collective-permute-start.2) | collective-permute-done | bytes 65568 | tf_op jit(solution)/shard_map/ppermute | solution.py:395
  81.2 1.6 collective-permute-start.9
  84.2 40.8 %shard_map.158 = (f32[32,2048]{1,0:T(8,128)S(1)}, bf16[16,32,2048]{2,1,0:T(8,128)(2,1)S(1)}) custom-call(f32[16,32,1024]{2,1,0:T(8,128)S(1)} %bitcast.96, f32[16,32,1024]{2,1,0:T(8,128)S(1)} %bitcast.98, f32[32,2048]{1,0:T(8,128)S(1)} %fusion.67.refs_2_, f32[1,2048]{1,0:T(1,128)S(1)} %bitcast.104), custom_call_target="tpu_custom_call" | custom-call | flops 10000000 | bytes 100000000 | tf_op jit(solution)/shard_map/pallas_call | solution.py:167
  125.0 1.7 fusion.35
  127.3 1.8 fusion.55
  129.1 1.7 fusion.33
  130.8 1.6 collective-permute-start.10
  132.4 1.6 fusion.12
  134.0 1.8 fusion.91
  135.8 1.8 fusion.92
  137.7 43.0 %shard_map.159 = (f32[32,2048]{1,0:T(8,128)}, bf16[16,32,2048]{2,1,0:T(8,128)(2,1)S(1)}) custom-call(f32[16,32,1024]{2,1,0:T(8,128)S(1)} %bitcast.97, f32[16,32,1024]{2,1,0:T(8,128)S(1)} %bitcast.99, f32[32,2048]{1,0:T(8,128)S(1)} %get-tuple-element.8.refs_2_, f32[1,2048]{1,0:T(1,128)S(1)} %bitcast.105), custom_call_target="tpu_custom_call" | custom-call | flops 10000000 | bytes 100000000 | tf_op jit(solution)/shard_map/pallas_call | solution.py:167
  188.4 13.6 %score.1 = (f32[4,128]{1,0:T(4,128)}, f32[8,128]{1,0:T(8,128)}) custom-call(s32[2]{0:T(128)} %counts.1, f32[8,128]{1,0:T(8,128)} %reshape.278.mine), custom_call_target="tpu_custom_call" | custom-call | flops 1000 | bytes 10000000 | tf_op jit(solution)/shard_map/score/pallas_call | solution.py:266
  (91 shorter events, 21.9 us)
Async XLA Ops:
  0.6 4.7 %copy-start.1 = (bf16[2,128,2048]{2,1,0:T(8,128)(2,1)S(1)}, bf16[2,128,2048]{2,1,0:T(8,128)(2,1)}, u32[]{:S(2)}) copy-start(bf16[2,128,2048]{2,1,0:T(8,128)(2,1)} %param.17) | copy-start | bytes 3145732
  0.6 26.7 %collective-permute-start = (bf16[1024,128]{1,0:T(8,128)(2,1)}, bf16[1024,128]{1,0:T(8,128)(2,1)}, u32[]{:S(2)}, u32[]{:S(2)}) collective-permute-start(bf16[1024,128]{1,0:T(8,128)(2,1)} %param.22), channel_id=1, source_target_pairs={{1,0},{0,1},{3,2},{2,3},{5,4},{4,5},{7,6},{6,7},{9,8},{8,9},{11,10... | collective-permute-start | bytes 786440 | tf_op jit(solution)/shard_map/ppermute | solution.py:319
  7.3 58.8 %all-to-all-start = ((bf16[16,2,128,128]{2,3,1,0:T(8,128)(2,1)}), bf16[16,2,128,128]{2,3,1,0:T(8,128)(2,1)S(1)}, u32[]{:S(2)}, u32[]{:S(2)}) async-start(bf16[16,2,128,128]{2,3,1,0:T(8,128)(2,1)} %copy.34), calls=%async_computation | async-start | bytes 2097152 | tf_op jit(solution)/shard_map/all_to_all | solution.py:351
  13.2 68.0 %collective-permute-start.3 = (bf16[128,1024]{1,0:T(8,128)(2,1)}, bf16[128,1024]{1,0:T(8,128)(2,1)}, u32[]{:S(2)}, u32[]{:S(2)}) collective-permute-start(bf16[128,1024]{1,0:T(8,128)(2,1)} %param.23), channel_id=1, source_target_pairs={{1,0},{0,1},{3,2},{2,3},{5,4},{4,5},{7,6},{6,7},{9,8},{8,9},{11,10... | collective-permute-start | bytes 786440 | tf_op jit(solution)/shard_map/ppermute | solution.py:319
  13.8 112.9 %collective-permute-start.4 = (bf16[1024,320]{0,1:T(8,128)(2,1)}, bf16[1024,320]{0,1:T(8,128)(2,1)}, u32[]{:S(2)}, u32[]{:S(2)}) collective-permute-start(bf16[1024,320]{0,1:T(8,128)(2,1)} %param.25), channel_id=1, source_target_pairs={{1,0},{0,1},{3,2},{2,3},{5,4},{4,5},{7,6},{6,7},{9,8},{8,9},{11,10... | collective-permute-start | bytes 1966088 | tf_op jit(solution)/shard_map/ppermute | solution.py:319
  15.3 115.5 %collective-permute-start.5 = (bf16[1024,320]{0,1:T(8,128)(2,1)}, bf16[1024,320]{0,1:T(8,128)(2,1)}, u32[]{:S(2)}, u32[]{:S(2)}) collective-permute-start(bf16[1024,320]{0,1:T(8,128)(2,1)} %param.26), channel_id=1, source_target_pairs={{1,0},{0,1},{3,2},{2,3},{5,4},{4,5},{7,6},{6,7},{9,8},{8,9},{11,10... | collective-permute-start | bytes 1966088 | tf_op jit(solution)/shard_map/ppermute | solution.py:319
  15.8 120.0 %collective-permute-start.6 = (bf16[320,1024]{1,0:T(8,128)(2,1)}, bf16[320,1024]{1,0:T(8,128)(2,1)}, u32[]{:S(2)}, u32[]{:S(2)}) collective-permute-start(bf16[320,1024]{1,0:T(8,128)(2,1)} %param.27), channel_id=1, source_target_pairs={{1,0},{0,1},{3,2},{2,3},{5,4},{4,5},{7,6},{6,7},{9,8},{8,9},{11,10... | collective-permute-start | bytes 1966088 | tf_op jit(solution)/shard_map/ppermute | solution.py:319
  19.0 0.7 copy-start.7
  19.8 3.6 %copy-start.9 = (f32[2048]{0:T(1024)S(1)}, f32[2048]{0:T(1024)}, u32[]{:S(2)}) copy-start(f32[2048]{0:T(1024)} %param.28) | copy-start | bytes 24580
  19.8 3.6 %copy-start.10 = (f32[2048]{0:T(1024)S(1)}, f32[2048]{0:T(1024)}, u32[]{:S(2)}) copy-start(f32[2048]{0:T(1024)} %param.24) | copy-start | bytes 24580
  19.8 3.6 %copy-start.8 = (s32[2,8,32]{2,1,0:T(8,128)S(1)}, s32[2,8,32]{2,1,0:T(8,128)}, u32[]{:S(2)}) copy-start(s32[2,8,32]{2,1,0:T(8,128)} %param.20) | copy-start | bytes 6148
  23.4 2.4 %copy-start.11 = (s32[2]{0:T(128)S(1)}, s32[2]{0:T(128)}, u32[]{:S(2)}) copy-start(s32[2]{0:T(128)} %param.18) | copy-start | bytes 28
  25.9 1.0 copy-start.6
  28.8 36.8 %collective-permute-start.1 = (bf16[512,64]{0,1:T(8,128)(2,1)S(1)}, bf16[512,64]{0,1:T(8,128)(2,1)S(1)}, u32[]{:S(2)}, u32[]{:S(2)}) collective-permute-start(bf16[512,64]{0,1:T(8,128)(2,1)S(1)} %get-tuple-element.30), channel_id=1, source_target_pairs={{1,0},{0,1},{3,2},{2,3},{5,4},{4,5},{7,6},{6,7},{9,8},{8,9},{11,10... | collective-permute-start | bytes 196616 | tf_op jit(solution)/shard_map/ppermute | solution.py:319
  70.9 8.3 %copy-start.4 = (bf16[1024,504]{0,1:T(8,128)(2,1)S(1)}, bf16[1024,504]{0,1:T(8,128)(2,1)}, u32[]{:S(2)}) copy-start(bf16[1024,504]{0,1:T(8,128)(2,1)} %get-tuple-element.21) | copy-start | bytes 3096580
  74.6 6.6 %copy-start.3 = (bf16[1024,504]{0,1:T(8,128)(2,1)S(1)}, bf16[1024,504]{0,1:T(8,128)(2,1)}, u32[]{:S(2)}) copy-start(bf16[1024,504]{0,1:T(8,128)(2,1)} %get-tuple-element.22) | copy-start | bytes 3096580
  74.9 4.3 %collective-permute-start.2 = (bf16[512,64]{0,1:T(8,128)(2,1)S(1)}, bf16[512,64]{0,1:T(8,128)(2,1)S(1)}, u32[]{:S(2)}, u32[]{:S(2)}) collective-permute-start(bf16[512,64]{0,1:T(8,128)(2,1)S(1)} %bitcast.113), channel_id=1, source_target_pairs={{0,1},{1,0},{2,3},{3,2},{4,5},{5,4},{6,7},{7,6},{8,9},{9,8},{10,11... | collective-permute-start | bytes 196616 | tf_op jit(solution)/shard_map/ppermute | solution.py:395
  79.3 105.4 %collective-permute-start.7 = (bf16[1024,504]{0,1:T(8,128)(2,1)S(1)}, bf16[1024,504]{0,1:T(8,128)(2,1)S(1)}, u32[]{:S(2)}, u32[]{:S(2)}) collective-permute-start(bf16[1024,504]{0,1:T(8,128)(2,1)S(1)} %copy-done.4), channel_id=1, source_target_pairs={{1,0},{0,1},{3,2},{2,3},{5,4},{4,5},{7,6},{6,7},{9,8},{8,9},{11,10... | collective-permute-start | bytes 3096584 | tf_op jit(solution)/shard_map/ppermute | solution.py:319
  81.2 104.2 %collective-permute-start.9 = (bf16[1024,504]{0,1:T(8,128)(2,1)S(1)}, bf16[1024,504]{0,1:T(8,128)(2,1)S(1)}, u32[]{:S(2)}, u32[]{:S(2)}) collective-permute-start(bf16[1024,504]{0,1:T(8,128)(2,1)S(1)} %copy-done.3), channel_id=1, source_target_pairs={{1,0},{0,1},{3,2},{2,3},{5,4},{4,5},{7,6},{6,7},{9,8},{8,9},{11,10... | collective-permute-start | bytes 3096584 | tf_op jit(solution)/shard_map/ppermute | solution.py:319
  124.9 1.7 copy-start.2
  126.7 59.5 %collective-permute-start.8 = (bf16[1024,504]{0,1:T(8,128)(2,1)S(1)}, bf16[1024,504]{0,1:T(8,128)(2,1)S(1)}, u32[]{:S(2)}, u32[]{:S(2)}) collective-permute-start(bf16[1024,504]{0,1:T(8,128)(2,1)S(1)} %copy-done.2), channel_id=1, source_target_pairs={{1,0},{0,1},{3,2},{2,3},{5,4},{4,5},{7,6},{6,7},{9,8},{8,9},{11,10... | collective-permute-start | bytes 3096584 | tf_op jit(solution)/shard_map/ppermute | solution.py:319
  129.1 1.7 copy-start.5
  130.8 50.6 %collective-permute-start.10 = (bf16[1024,496]{0,1:T(8,128)(2,1)S(1)}, bf16[1024,496]{0,1:T(8,128)(2,1)S(1)}, u32[]{:S(2)}, u32[]{:S(2)}) collective-permute-start(bf16[1024,496]{0,1:T(8,128)(2,1)S(1)} %copy-done.5), channel_id=1, source_target_pairs={{1,0},{0,1},{3,2},{2,3},{5,4},{4,5},{7,6},{6,7},{9,8},{8,9},{11,10... | collective-permute-start | bytes 3047432 | tf_op jit(solution)/shard_map/ppermute | solution.py:319
  137.6 43.1 %copy-start = (bf16[1024,2008]{0,1:T(8,128)(2,1)S(1)}, bf16[1024,2008]{0,1:T(8,128)(2,1)}, u32[]{:S(2)}) copy-start(bf16[1024,2008]{0,1:T(8,128)(2,1)} %param.29) | copy-start | bytes 12337156
